TPU v7x, 32 devices: a 4x2x2 block of a 4x4x8 slice. The times are simulated.
32 devices in a mesh: model: 4 (over y, z), data: 8 (over x, core).
Axes of the slice: x: 4, y: 2, z: 2, core: 2. Of those that a mesh axis runs over, the one named last changes fastest.
The devices are a block of a 4x4x8 slice.
Arguments:
- grad_sq: float32 [32, 12, 256, 256], P(('model', 'data')), parts along dimension 0
- mom_sq: float32 [48, 256, 256], P('model', 'data'), parts along dimension 0
- weight_sq: float32 [48, 256, 256], P('model', 'data'), parts along dimension 0
- grad_kv: float32 [32, 12, 256, 64], P(('model', 'data')), parts along dimension 0
- mom_kv: float32 [48, 256, 64], P('model', 'data'), parts along dimension 0
- weight_kv: float32 [48, 256, 64], P('model', 'data'), parts along dimension 0
- grad_up: float32 [32, 12, 256, 1024], P(('model', 'data')), parts along dimension 0
- mom_up: float32 [48, 256, 1024], P('model', 'data'), parts along dimension 0
- weight_up: float32 [48, 256, 1024], P('model', 'data'), parts along dimension 0
- grad_down: float32 [32, 6, 1024, 256], P(('model', 'data')), parts along dimension 0
- mom_down: float32 [24, 1024, 256], P('model', 'data'), parts along dimension 0
- weight_down: float32 [24, 1024, 256], P('model', 'data'), parts along dimension 0
Outputs:
- output 1: float32 [48, 256, 256], P('model', 'data'), parts along dimension 0
- output 2: float32 [48, 256, 256], P('model', 'data'), parts along dimension 0
- output 3: bfloat16 [48, 256, 256], P('model'), parts along dimension 0
- output 4: float32 [48, 256, 64], P('model', 'data'), parts along dimension 0
- output 5: float32 [48, 256, 64], P('model', 'data'), parts along dimension 0
- output 6: bfloat16 [48, 256, 64], P('model'), parts along dimension 0
- output 7: float32 [48, 256, 1024], P('model', 'data'), parts along dimension 0
- output 8: float32 [48, 256, 1024], P('model', 'data'), parts along dimension 0
- output 9: bfloat16 [48, 256, 1024], P('model'), parts along dimension 0
- output 10: float32 [24, 1024, 256], P('model', 'data'), parts along dimension 0
- output 11: float32 [24, 1024, 256], P('model', 'data'), parts along dimension 0
- output 12: bfloat16 [24, 1024, 256], P('model'), parts along dimension 0
There are 4 independent parts. A program takes and returns all parts, laid end to end along the dimension named above; each array names one.
All inputs are finite; a program needn't handle non-finite values.
Results may differ from a plain program's by a relative error of at most 0.00957222.
Values are sent between devices in bfloat16 or wider.
A program may use at most 768 MiB of HBM per device.

v0:
```python
import math

import jax
import jax.numpy as jnp
from jax import lax
from jax.experimental import pallas as pl
from jax.experimental.pallas import tpu as pltpu
from jax.sharding import PartitionSpec as P

NS_STEPS = 5
MU = 0.95
LR = 0.1
WD = 0.5
EPS = 1e-7
COEF_A = 3.4445
COEF_B = -4.7750
COEF_C = 2.0315
F32 = jnp.float32
BF16 = jnp.bfloat16
MESH = pl.DeviceIdType.MESH
NT = (((1,), (1,)), ((), ()))
PACK = 4

PIECES = (
    ("u", 0, 1, 2), ("u", 2, 3, 4), ("u", 4, 5, 6), ("u", 6, 7, 8), ("u", 8, 9, 10), ("u", 10, 11, 12),
    ("w", 0, 1, 2), ("w", 2, 3, 4), ("w", 4, 5, 6), ("s", 0, 4, 8), ("s", 8, 12, 15),
)
GROUPS = (
    ("u", 0, 2, 4), ("u", 4, 6, 8), ("u", 8, 10, 12), ("w", 0, 2, 4), ("w", 4, 5, 6), ("s", 0, 4, 8), ("s", 8, 11, 15),
)
OWNER = {
    "u": tuple((dev, 0) for dev in (0, 2, 4, 6, 1, 3, 5, 7)) + tuple((dev, 1) for dev in (0, 2, 4, 6)),
    "w": tuple((dev, 0) for dev in (1, 3, 5, 7)) + ((0, 1), (2, 1)),
    "s": tuple((dev, slot) for dev in (4, 5, 6, 7, 1, 3) for slot in (0, 1)) + ((4, 2), (5, 2), (6, 2)),
}
PEER_SETS = ((1,), (2,), (3, 4, 5), (6, 7, 8), (9, 10))
U_AFTER = {1: (0, 1), 3: (2, 3), 5: (4, 5), 7: (6, 7), 9: (8, 9), 10: (10,)}
SLOT = {"u": 0, "w": 2, "s": 4}


def muon_kernel(n, nx, sq_count, *refs):
    (g_sq, g_kv, g_up, g_dn, m_sq, m_kv, m_up, m_dn, w_sq, w_kv, w_up, w_dn,
     mv_s, wv_s, f_s, mv_k, wv_k, fk, mv_u, wv_u, f_u, mv_w, wv_w, f_w,
     p_s, p_u, p_w, q_s, q_u, q_w, pk, qk,
     t_s, t_u, t_w, l_s, l_u, l_w, r_s, r_u, r_w,
     us_s, us_u, us_w, uo_s, uo_u, uo_w, xr_s, xr_u, xr_w, xt, xs, first,
     sem_load, sem_mw, sem_peer_s, sem_peer_r, sem_first, sem_st_s, sem_opp, sem_fin, sem_us, sem_ur,
     sem_xs, sem_xr, sem_gs, sem_gr) = refs
    part = {"s": p_s, "u": p_u, "w": p_w}
    other = {"s": q_s, "u": q_u, "w": q_w}
    opp = {"s": t_s, "u": t_u, "w": t_w}
    from_l = {"s": l_s, "u": l_u, "w": l_w}
    from_r = {"s": r_s, "u": r_u, "w": r_w}
    grad = {"s": g_sq, "u": g_up, "w": g_dn}
    mom = {"s": mv_s, "u": mv_u, "w": mv_w}
    wei = {"s": wv_s, "u": wv_u, "w": wv_w}
    u_send = {"s": us_s, "u": us_u, "w": us_w}
    u_own = {"s": uo_s, "u": uo_u, "w": uo_w}
    x_recv = {"s": xr_s, "u": xr_u, "w": xr_w}
    full = {"s": f_s, "u": f_u, "w": f_w}
    scale = {
        "s": 0.2 * math.sqrt(n * m_sq.shape[1]),
        "u": 0.2 * math.sqrt(m_up.shape[2]),
        "w": 0.2 * math.sqrt(n * m_dn.shape[1]),
    }

    d = lax.axis_index("data")
    x = d // 2
    c = lax.rem(d, 2)
    xr = lax.rem(x + 1, nx)
    xl = lax.rem(x + nx - 1, nx)
    xo = lax.rem(x + 2, nx)
    right, left, peer = 2 * xr + c, 2 * xl + c, 2 * x + 1 - c

    def remote(src, dst, ssem, rsem, dev):
        return pltpu.make_async_remote_copy(
            src_ref=src, dst_ref=dst, send_sem=ssem, recv_sem=rsem, device_id={"data": dev}, device_id_type=MESH)

    def arrived(dst, rsem):
        remote(dst, dst, sem_gs.at[0], rsem, peer).wait_recv()

    def drained(src, ssem):
        remote(src, src, ssem, sem_xr.at[0], peer).wait_send()

    def loaded(dst, sem):
        pltpu.make_async_copy(dst, dst, sem).wait()

    def send(src, dst, ssem, rsem, dev):
        remote(src, dst, ssem, rsem, dev).start()

    fams = ("u", "w", "s")

    def piece(p):
        f, j0, _, j1 = PIECES[p]
        return f, pl.ds(j0, (min(j1, sq_count) if f == "s" else j1) - j0)

    def load_part(p):
        f, r = piece(p)
        pltpu.make_async_copy(grad[f].at[r, :, c], part[f].at[r], sem_load.at[1 + fams.index(f) if p else 0]).start()

    f0, r0 = piece(0)
    pltpu.make_async_copy(grad[f0].at[r0, :, 1 - c], first, sem_load.at[5]).start()
    barrier = pltpu.get_barrier_semaphore()
    for dev in (left, right, peer):
        pl.semaphore_signal(barrier, inc=1, device_id={"data": dev}, device_id_type=MESH)
    load_part(0)
    pl.semaphore_wait(barrier, 3)
    loaded(first, sem_load.at[5])
    for i, to in enumerate((xo, xr, xl, x)):
        send(first.at[:, to], other[f0].at[r0, to], sem_peer_s.at[fams.index(f0)], sem_first.at[i], peer)

    for p in range(1, len(PIECES)):
        f, r = piece(p)
        load_part(p)
        send(grad[f].at[r, :, 1 - c], other[f].at[r], sem_peer_s.at[fams.index(f)],
             sem_peer_r.at[next(i for i, pieces in enumerate(PEER_SETS) if p in pieces)], peer)
    pltpu.make_async_copy(g_kv, pk, sem_load.at[4]).start()
    send(g_kv, qk, sem_peer_s.at[3], sem_peer_r.at[len(PEER_SETS)], peer)
    sq = pl.ds(0, sq_count)
    for i, src, dst in ((0, m_up, mv_u), (0, w_up, wv_u), (1, m_dn, mv_w), (1, w_dn, wv_w),
                        (2, m_sq, mv_s.at[sq]), (2, w_sq, wv_s), (3, m_kv, mv_k), (4, w_kv, wv_k)):
        pltpu.make_async_copy(src, dst, sem_mw.at[i]).start()
    first_n = PIECES[0][3]
    pending = {
        "load_u": lambda: loaded(part["u"].at[pl.ds(first_n, p_u.shape[0] - first_n)], sem_load.at[1]),
        "load_w": lambda: loaded(part["w"], sem_load.at[2]),
        "load_s": lambda: loaded(part["s"].at[sq], sem_load.at[3]),
        "mom_u": lambda: loaded(part["u"].at[:, pl.ds(0, 2)], sem_mw.at[0]),
        "mom_w": lambda: loaded(part["w"].at[:, pl.ds(0, 2)], sem_mw.at[1]),
        "mom_s": lambda: loaded(part["s"].at[sq, pl.ds(0, 2)], sem_mw.at[2]),
    }

    def need(key):
        if key in pending:
            pending.pop(key)()

    def exchange(pieces, i):
        f, j0, _, _ = PIECES[pieces[0]]
        j1 = PIECES[pieces[-1]][3]
        return lambda: arrived(other[f].at[pl.ds(j0, (min(j1, sq_count) if f == "s" else j1) - j0)], sem_peer_r.at[i])

    for i, pieces in enumerate(PEER_SETS):
        pending[pieces] = exchange(pieces, i)

    def stage_a(p):
        f, j0, jm, j1 = PIECES[p]
        e1 = min(j1, sq_count) if f == "s" else j1
        if p == 0:
            loaded(part[f].at[pl.ds(j0, j1 - j0)], sem_load.at[0])
        else:
            need("load_" + f)
        pr, ot = part[f], other[f]
        a, b = pl.ds(j0, jm - j0), pl.ds(jm, j1 - jm)

        def send_opp():
            send(pr.at[a, xo], opp[f].at[a], sem_st_s.at[fams.index(f)], sem_opp.at[p], right)
            send(pr.at[b, xo], opp[f].at[b], sem_st_s.at[fams.index(f)], sem_opp.at[p], left)

        def send_right():
            send(pr.at[b, xr], from_l[f].at[b], sem_st_s.at[fams.index(f)], sem_fin.at[p], right)

        def send_left():
            send(pr.at[a, xl], from_r[f].at[a], sem_st_s.at[fams.index(f)], sem_fin.at[p], left)

        if p == 0:
            for i, (to, then) in enumerate(((xo, send_opp), (xr, send_right), (xl, send_left), (x, None))):
                arrived(ot.at[pl.ds(j0, j1 - j0), to], sem_first.at[i])

                def add_first(j, carry):
                    pr[j, to] = pr[j, to] + ot[j, to]
                    return carry
                lax.fori_loop(j0, j1, add_first, 0)
                if then is not None:
                    then()
            return
        need(next(pieces for pieces in PEER_SETS if p in pieces))
        if f == "s":
            def add(j, carry):
                pr[j] = pr[j] + ot[j]
                return carry
            lax.fori_loop(j0, e1, add, 0)
            if j1 > sq_count:
                loaded(pk, sem_load.at[4])
                arrived(qk, sem_peer_r.at[len(PEER_SETS)])
                rows, lanes = p_s.shape[2], p_s.shape[3]
                for i in range(j1 - sq_count):
                    t = jnp.transpose(pk[i] + qk[i]).reshape(nx, 2, rows, lanes)
                    pr[sq_count + i] = jnp.where(c == 0, t[:, 0], t[:, 1])
        else:
            def add(t, carry):
                j, xi = j0 + t // nx, lax.rem(t, nx)
                pr[j, xi] = pr[j, xi] + ot[j, xi]
                return carry
            lax.fori_loop(0, (j1 - j0) * nx, add, 0)
        send_opp()
        send_right()
        send_left()

    def stage_b(p):
        f, j0, jm, j1 = PIECES[p]
        op, pr = opp[f], part[f]
        arrived(op.at[pl.ds(j0, j1 - j0)], sem_opp.at[p])
        for lo, hi, to, dev, dst in ((j0, jm, xr, right, from_l), (jm, j1, xl, left, from_r)):
            r = pl.ds(lo, hi - lo)

            def add(j, carry):
                op[j] = op[j] + pr[j, to]
                return carry
            lax.fori_loop(lo, hi, add, 0)
            send(op.at[r], dst[f].at[r], sem_st_s.at[fams.index(f)], sem_fin.at[p], dev)

    def by_count(devs, fn):
        counts = [devs.count(dev) for dev in range(n)]
        for k in sorted(set(counts)):
            mine = d == counts.index(k)
            for dev in range(counts.index(k) + 1, n):
                if counts[dev] == k:
                    mine = mine | (d == dev)
            pl.when(mine)(lambda k=k: fn(k))

    def u_drained():
        for i, f in enumerate(fams):
            total = len(OWNER[f])
            by_count([dev for dev, _ in OWNER[f]], lambda k: drained(u_send[f].at[pl.ds(0, total - k)], sem_us.at[i]))

    def stage_c(p):
        f, j0, jm, j1 = PIECES[p]
        need("mom_" + f)
        arrived(part[f].at[pl.ds(j0, j1 - j0), pl.ds(0, 2)], sem_fin.at[p])
        if j1 > sq_count:
            loaded(mv_k, sem_mw.at[3])
            wide = m_kv.shape[2]
            for i in range(j1 - sq_count):
                mv_s[sq_count + i] = jnp.concatenate([mv_k[PACK * i + k] for k in range(PACK)], axis=-1)

        def update(j, carry):
            g = ((part[f][j, x] + from_l[f][j]) + from_r[f][j]) * (1.0 / n)
            m = MU * mom[f][j] + g
            mom[f][j] = m
            u_send[f][j] = (g + MU * m).astype(BF16)
            return carry
        lax.fori_loop(j0, j1, update, 0)
        for ready in U_AFTER.get(p, ()):
            rf, r0, _, r1 = PIECES[ready]
            for j in range(r0, r1):
                dev, slot = OWNER[rf][j]
                copy = remote(u_send[rf].at[j], u_own[rf].at[slot, d], sem_us.at[fams.index(rf)],
                              sem_ur.at[SLOT[rf] + slot], dev)
                pl.when(d != dev)(copy.start)
        if j1 > sq_count:
            for i in range(j1 - sq_count):
                for k in range(PACK):
                    mv_k[PACK * i + k] = mv_s[sq_count + i, :, wide * k:wide * (k + 1)]

    def take(f, slot, j):
        rows = u_own[f].at[slot, pl.ds(0, n - 1)]
        arrived(rows, sem_ur.at[SLOT[f] + slot])
        u_own[f][slot, d] = u_send[f][j]

    def give(f, slot, j, q):
        for k in range(1, n):
            to = lax.rem(d + k, n)
            send(u_own[f].at[slot, to], x_recv[f].at[j], sem_xs.at[SLOT[f] + slot], sem_xr.at[q], to)
        x_recv[f][j] = u_own[f][slot, d]

    def given(f, slot):
        drained(u_own[f].at[slot, pl.ds(0, n - 1)], sem_xs.at[SLOT[f] + slot])

    xt_rows = xt.shape[1]

    def frob(ref):
        def square(i, acc):
            v = ref[i].astype(F32)
            return acc + v * v
        total = lax.fori_loop(0, n, square, jnp.zeros(ref.shape[1:], F32))
        return jnp.sqrt(jnp.sum(total, axis=(0, 1), keepdims=True)) + EPS

    def start_up(slot):
        ref = u_own["u"].at[slot]
        norm = frob(ref)
        for i in range(n):
            xt[i] = (ref[i].astype(F32) / norm).astype(BF16)

    def end_up(slot):
        for i in range(n):
            u_own["u"][slot, i] = xt[i]

    def start_dn(slot):
        ref = u_own["w"].at[slot]
        norm = frob(ref)
        width = ref.shape[1]
        for i in range(n):
            t = jnp.transpose(ref[i].astype(F32) / norm).astype(BF16)
            xt[:, :, width * i:width * (i + 1)] = t.reshape(n, xt_rows, width)

    def end_dn(slot):
        width = u_own["w"].shape[2]
        for i in range(n):
            t = xt[:, :, width * i:width * (i + 1)].reshape(n * xt_rows, width)
            u_own["w"][slot, i] = jnp.transpose(t.astype(F32)).astype(BF16)

    def ns_large():
        k, l = n * xt_rows, xt.shape[2]

        def step(_, carry):
            v = xt[...].reshape(k, l)
            gram = lax.dot_general(v, v, NT, preferred_element_type=F32).astype(BF16)
            square = jnp.dot(gram, gram, preferred_element_type=F32)
            poly = (COEF_B * gram.astype(F32) + COEF_C * square).astype(BF16)
            for i in range(0, l, k):
                v = xt[:, :, i:i + k].reshape(k, k)
                y = COEF_A * v.astype(F32) + jnp.dot(poly, v, preferred_element_type=F32)
                xt[:, :, i:i + k] = y.astype(BF16).reshape(n, xt_rows, k)
            return carry
        lax.fori_loop(0, NS_STEPS, step, 0)

    def ns_small(slots, mask):
        def step(_, carry):
            for s in slots:
                v = xs[s]
                gram = lax.dot_general(v, v, NT, preferred_element_type=F32)
                if mask is not None:
                    gram = jnp.where(mask, gram, 0.0)
                gram = gram.astype(BF16)
                square = jnp.dot(gram, gram, preferred_element_type=F32)
                poly = (COEF_B * gram.astype(F32) + COEF_C * square).astype(BF16)
                xs[s] = (COEF_A * v.astype(F32) + jnp.dot(poly, v, preferred_element_type=F32)).astype(BF16)
            return carry
        lax.fori_loop(0, NS_STEPS, step, 0)

    up_a = x + c * nx
    up_b = n + x
    even = c == 0

    def round_a():
        take("u", 0, up_a)
        start_up(0)
        ns_large()
        end_up(0)
        give("u", 0, up_a, c)

    half = n // 2

    def round_b():
        @pl.when(even)
        def _():
            take("u", 1, up_b)
            start_up(1)

        @pl.when(jnp.logical_not(even))
        def _():
            take("w", 0, x)
            start_dn(0)
        ns_large()

        @pl.when(even)
        def _():
            end_up(1)
            give("u", 1, up_b, 2)

        @pl.when(jnp.logical_not(even))
        def _():
            end_dn(0)
            give("w", 0, x, 3)

    has_dn = (d == 0) | (d == 2)
    has_kv = (d >= half) & (d < n - 1)
    dn_j = nx + x
    sq_j = 2 * jnp.where(d < half, half + x, d - half)
    kv_j = sq_count + d - half

    def round_c():
        @pl.when(has_dn)
        def _():
            take("w", 1, dn_j)
            start_dn(1)
            ns_large()
            end_dn(1)
            give("w", 1, dn_j, 4)

        size = xs.shape[1]

        @pl.when(jnp.logical_not(has_dn))
        def _():
            for s in range(2):
                take("s", s, sq_j + s)
                norm = frob(u_own["s"].at[s])
                xs[s] = (u_own["s"][s].astype(F32) / norm).astype(BF16).reshape(size, size)
            ns_small((0, 1), None)
            for s in range(2):
                u_own["s"][s] = xs[s].reshape(n, size // n, size)
                give("s", s, sq_j + s, jnp.where(d < half, 6, 5))

        @pl.when(has_kv)
        def _():
            take("s", 2, kv_j)
            u = jnp.transpose(u_own["s"][2].astype(F32).reshape(size, size))
            wide = size // PACK
            rows = jnp.sum(u * u, axis=1, keepdims=True)
            norm = jnp.concatenate(
                [jnp.broadcast_to(jnp.sum(rows[wide * k:wide * (k + 1)], axis=0, keepdims=True), (wide, 1))
                 for k in range(PACK)], axis=0)
            xs[2] = (u / (jnp.sqrt(norm) + EPS)).astype(BF16)
            mask = (lax.broadcasted_iota(jnp.int32, (size, size), 0) // wide
                    == lax.broadcasted_iota(jnp.int32, (size, size), 1) // wide)
            ns_small((2,), mask)
            u_own["s"][2] = jnp.transpose(xs[2].astype(F32)).astype(BF16).reshape(n, size // n, size)
            give("s", 2, kv_j, 6)

    def stage_d(q):
        f, j0, jm, j1 = GROUPS[q]
        by_count([dev for dev, _ in OWNER[f][j0:j1]],
                 lambda k: arrived(x_recv[f].at[pl.ds(j0, j1 - j0 - k)], sem_xr.at[q]))
        if j1 > sq_count:
            loaded(wv_k, sem_mw.at[4])
        e1 = min(j1, sq_count) if f == "s" else j1

        def update(j, carry):
            w = wei[f][j]
            w = w - LR * (scale[f] * x_recv[f][j].astype(F32) + WD * w)
            wei[f][j] = w
            full[f][j, d] = w.astype(BF16)
            return carry
        lax.fori_loop(j0, e1, update, 0)
        if j1 > sq_count:
            wide = w_kv.shape[2]
            for i in range(j1 - sq_count):
                w = jnp.concatenate([wv_k[PACK * i + k] for k in range(PACK)], axis=-1)
                w = w - LR * (scale[f] * x_recv[f][sq_count + i].astype(F32) + WD * w)
                full[f][sq_count + i, d] = w.astype(BF16)
                for k in range(PACK):
                    wv_k[PACK * i + k] = w[:, wide * k:wide * (k + 1)]
        mine = full[f].at[pl.ds(j0, j1 - j0), d]
        send(mine, mine, sem_gs.at[fams.index(f)], sem_gr.at[q, 0], right)
        send(mine, mine, sem_gs.at[fams.index(f)], sem_gr.at[q, 0], left)
        send(mine, mine, sem_gs.at[fams.index(f)], sem_gr.at[q, 2], peer)

    def stage_e(q):
        f, j0, jm, j1 = GROUPS[q]
        a, b, r = pl.ds(j0, jm - j0), pl.ds(jm, j1 - jm), pl.ds(j0, j1 - j0)
        arrived(full[f].at[r, pl.ds(0, 2)], sem_gr.at[q, 0])
        for near, half_r, dev in ((left, a, right), (right, b, left)):
            send(full[f].at[half_r, near], full[f].at[half_r, near], sem_gs.at[fams.index(f)], sem_gr.at[q, 1], dev)
            send(full[f].at[r, near], full[f].at[r, near], sem_gs.at[fams.index(f)], sem_gr.at[q, 2], peer)

    def stage_h(q):
        f, j0, jm, j1 = GROUPS[q]
        block = full[f].at[pl.ds(j0, j1 - j0), 2 * xo + c]
        arrived(block, sem_gr.at[q, 1])
        send(block, block, sem_gs.at[fams.index(f)], sem_gr.at[q, 2], peer)

    def stage_z(q):
        f, j0, jm, j1 = GROUPS[q]
        r = pl.ds(j0, j1 - j0)
        arrived(full[f].at[r, pl.ds(0, 4)], sem_gr.at[q, 2])
        if j1 > sq_count:
            size = fk.shape[1]
            for i in range(j1 - sq_count):
                fk[i] = jnp.transpose(full[f][sq_count + i].astype(F32).reshape(size, size)).astype(BF16)

    def scoped(name, fn):
        def run(*args):
            with jax.named_scope("_".join([name] + [str(a) for a in args])):
                fn(*args)
        return run

    stage_a, stage_b, stage_c = scoped("reduce_a", stage_a), scoped("reduce_b", stage_b), scoped("update_c", stage_c)
    stage_d, stage_e = scoped("weights_d", stage_d), scoped("forward_e", stage_e)
    stage_h, stage_z = scoped("across_h", stage_h), scoped("finish_z", stage_z)
    round_a, round_b, round_c = scoped("round_a", round_a), scoped("round_b", round_b), scoped("round_c", round_c)

    def reduced():
        for i, f in enumerate(fams):
            drained(part[f].at[:, pl.ds(0, 3)], sem_st_s.at[i])

    def exchanged():
        drained(part["u"], sem_peer_s.at[0])
        drained(part["w"], sem_peer_s.at[1])
        drained(part["s"].at[sq], sem_peer_s.at[2])
        drained(pk, sem_peer_s.at[3])

    count = len(PIECES)
    after = {
        5: (round_a, exchanged),
        8: (lambda: stage_d(0), round_b, lambda: given("u", 0)),
        9: (lambda: stage_d(1),),
    }
    for i in range(-2, count):
        if i + 2 < count:
            stage_a(i + 2)
        if 0 <= i + 1 < count:
            stage_b(i + 1)
        if i >= 0:
            stage_c(i)
        for act in after.get(i, ()):
            act()
    stage_d(2)
    stage_d(3)
    stage_e(0)
    round_c()
    for q in (1, 2, 3):
        stage_e(q)
    stage_d(4)
    stage_h(0)
    stage_d(6)
    stage_d(5)
    reduced()
    u_drained()
    pl.when(even)(lambda: given("u", 1))
    pl.when(jnp.logical_not(even))(lambda: given("w", 0))
    stage_z(0)
    for q in (1, 2, 3):
        stage_h(q)
    for q in (4, 6, 5):
        stage_e(q)
    pl.when(has_dn)(lambda: given("w", 1))

    @pl.when(jnp.logical_not(has_dn))
    def _():
        given("s", 0)
        given("s", 1)
    pl.when(has_kv)(lambda: given("s", 2))
    for q in (1, 2, 3):
        stage_z(q)
    stage_h(4)
    stage_h(6)
    stage_z(4)
    stage_z(6)
    stage_h(5)
    stage_z(5)
    for i, f in enumerate(fams):
        drained(full[f].at[:, pl.ds(0, n - 1)], sem_gs.at[i])


def write_kernel(*refs):
    sources, results, sem = refs[:12], refs[12:24], refs[24]
    copies = []
    for src, dst in zip(sources, results):
        count = dst.shape[0]
        step = count if len(dst.shape) == 3 else max(1, count // 3)
        for j in range(0, count, step):
            r = pl.ds(j, step)
            copies.append(pltpu.make_async_copy(src.at[r], dst.at[r], sem))
    for copy in copies:
        copy.start()
    for copy in copies:
        copy.wait()


def solution(mesh):
    n = mesh.shape["data"]
    nx = n // 2
    grad_spec = P(("model", "data"))
    slab_spec = P("model", "data")
    full_spec = P("model")

    def local_step(g_sq, m_sq, w_sq, g_kv, m_kv, w_kv, g_up, m_up, w_up, g_dn, m_dn, w_dn):
        def split(g, rows):
            return g[0].reshape(g.shape[1], nx, 2, rows, g.shape[3])

        sq, up, dn, kv = m_sq.shape, m_up.shape, m_dn.shape, m_kv.shape
        size = sq[2]
        packs = kv[0] // PACK
        small = sq[0] + packs
        grads = (
            split(g_sq, sq[1]),
            jnp.swapaxes(g_kv[0], 1, 2).reshape(packs, size, size),
            split(g_up, up[1]),
            split(g_dn, dn[1]),
        )
        fam = ((small,) + sq[1:], up, dn)

        def per(lead, dtype):
            return [pltpu.VMEM((shape[0],) + lead + shape[1:], dtype) for shape in fam]

        def own(slots):
            return [pltpu.VMEM((slot, n) + shape[1:], BF16) for slot, shape in zip(slots, fam)]

        dma = pltpu.SemaphoreType.DMA
        pieces, groups = len(PIECES), len(GROUPS)
        scratch = (
            per((nx,), F32) + per((nx,), F32) + [pltpu.VMEM((packs, size, size), F32)] * 2
            + per((), F32) + per((), F32) + per((), F32)
            + per((), BF16) + own((3, 2, 2)) + per((), BF16)
            + [pltpu.VMEM((n,) + up[1:], BF16), pltpu.VMEM((3, size, size), BF16),
               pltpu.VMEM((PIECES[0][3], nx) + up[1:], F32)]
            + [dma((6,)), dma((5,)), dma((4,)), dma((6,)), dma((4,)), dma((3,)), dma((pieces,)), dma((pieces,)),
               dma((3,)), dma((7,)), dma((7,)), dma((groups,)), dma((3,)), dma((groups, 3))]
        )

        def whole(shape):
            return (shape[0], n) + shape[1:]

        sds = jax.ShapeDtypeStruct
        out_shape = (
            sds(sq, F32), sds(sq, F32), sds(whole(sq), BF16),
            sds(kv, F32), sds(kv, F32), sds((packs, size, size), BF16),
            sds(up, F32), sds(up, F32), sds(whole(up), BF16),
            sds(dn, F32), sds(dn, F32), sds(whole(dn), BF16),
        )
        held = (
            (fam[0], F32), (sq, F32), (whole(fam[0]), BF16),
            (kv, F32), (kv, F32), ((packs, size, size), BF16),
            (up, F32), (up, F32), (whole(up), BF16),
            (dn, F32), (dn, F32), (whole(dn), BF16),
        )
        anywhere = pl.BlockSpec(memory_space=pl.ANY)
        inside = pl.BlockSpec(memory_space=pltpu.VMEM)

        def body(*refs):
            muon_kernel(n, nx, sq[0], *refs)

        res = pl.pallas_call(
            body,
            out_shape=[pltpu.VMEM(shape, dtype) for shape, dtype in held],
            in_specs=[anywhere] * 12,
            out_specs=[inside] * 12,
            scratch_shapes=scratch,
            compiler_params=pltpu.CompilerParams(
                collective_id=0, has_side_effects=True, vmem_limit_bytes=44 * 1024 * 1024),
            name="muon",
        )(*grads, m_sq, m_kv, m_up, m_dn, w_sq, w_kv, w_up, w_dn)
        res = pl.pallas_call(
            write_kernel,
            out_shape=out_shape,
            in_specs=[inside] * 12,
            out_specs=[anywhere] * 12,
            scratch_shapes=[dma],
            compiler_params=pltpu.CompilerParams(vmem_limit_bytes=2 * 1024 * 1024),
            name="write",
        )(*(pltpu.with_memory_space_constraint(r, pltpu.VMEM) for r in res))
        res = list(res)
        res[2] = res[2].reshape(sq[0], size, size)
        res[5] = jnp.swapaxes(res[5].reshape(kv[0], kv[2], size), 1, 2)
        res[8] = res[8].reshape(up[0], n * up[1], up[2])
        res[11] = res[11].reshape(dn[0], n * dn[1], dn[2])
        return tuple(res)

    in_specs = (grad_spec, slab_spec, slab_spec) * 4
    out_specs = (slab_spec, slab_spec, full_spec) * 4
    return jax.shard_map(local_step, mesh=mesh, in_specs=in_specs, out_specs=out_specs, check_vma=False)
```

profile of v0, /device:TPU:81, one launch (start us, length us, event | category | flops | bytes accessed | tf_op | source)
XLA Modules:
  0.0 185.5 jit_solution(3029490347167470264)
XLA Ops:
  0.6 178.8 %muon.1 = (f32[15,32,256]{2,1,0:T(8,128)S(1)}, f32[12,32,256]{2,1,0:T(8,128)S(1)}, bf16[15,8,32,256]{3,2,1,0:T(8,128)(2,1)S(1)}, f32[12,32,64]{2,1,0:T(8,128)S(1...) custom-call(f32[12,4,2,32,256]{4,3,2,1,0:T(8,128)} %bitcast.16, ...), custom_call_target="tpu_custom_call" | custom-call | tf_op jit(solution)/shard_map/muon/pallas_call | solution.py:613
  179.4 6.0 %write.1 = (f32[12,32,256]{2,1,0:T(8,128)}, f32[12,32,256]{2,1,0:T(8,128)}, bf16[12,8,32,256]{3,2,1,0:T(8,128)(2,1)}, f32[12,32,64]{2,1,0:T(8,128)}, f32[12,32,6...) custom-call(f32[15,32,256]{2,1,0:T(8,128)S(1)} %get-tuple-element.36, ...), custom_call_target="tpu_custom_call" | custom-call | tf_op jit(solution)/shard_map/write/pallas_call | solution.py:623
where the time goes:
time: 186 us; the launch traced here: 185 us
  Pallas kernels  185 us (99%)
    pallas_call x1, Pallas kernels, local_step(): pl.pallas_call(body, out_shape=[pltpu.VMEM(shape, dtype) for shape, dtype...  179 us
    pallas_call x1, Pallas kernels, local_step(): pl.pallas_call(write_kernel, out_shape=out_shape, in_specs=[inside] * 12,...  6.01 us

commit v1 on v0

--- a/solution.py
+++ b/solution.py
@@ -28,6 +28,7 @@
 GROUPS = (
     ("u", 0, 2, 4), ("u", 4, 6, 8), ("u", 8, 10, 12), ("w", 0, 2, 4), ("w", 4, 5, 6), ("s", 0, 4, 8), ("s", 8, 11, 15),
 )
+LAST = (0, 0, 0, 1, 1, 2, 3)
 OWNER = {
     "u": tuple((dev, 0) for dev in (0, 2, 4, 6, 1, 3, 5, 7)) + tuple((dev, 1) for dev in (0, 2, 4, 6)),
     "w": tuple((dev, 0) for dev in (1, 3, 5, 7)) + ((0, 1), (2, 1)),
@@ -44,8 +45,9 @@
      p_s, p_u, p_w, q_s, q_u, q_w, pk, qk,
      t_s, t_u, t_w, l_s, l_u, l_w, r_s, r_u, r_w,
      us_s, us_u, us_w, uo_s, uo_u, uo_w, xr_s, xr_u, xr_w, xt, xs, first,
-     sem_load, sem_mw, sem_peer_s, sem_peer_r, sem_first, sem_st_s, sem_opp, sem_fin, sem_us, sem_ur,
-     sem_xs, sem_xr, sem_gs, sem_gr) = refs
+     sem_load, sem_mw, sem_peer_s, sem_peer_r, sem_first, sem_st_s, sem_opp, sem_fin, sem_ur, sem_xr, sem_gr,
+     sem_last) = refs
+    sem_xs, sem_gs = sem_ur, sem_peer_s
     part = {"s": p_s, "u": p_u, "w": p_w}
     other = {"s": q_s, "u": q_u, "w": q_w}
     opp = {"s": t_s, "u": t_u, "w": t_w}
@@ -221,7 +223,7 @@
     def u_drained():
         for i, f in enumerate(fams):
             total = len(OWNER[f])
-            by_count([dev for dev, _ in OWNER[f]], lambda k: drained(u_send[f].at[pl.ds(0, total - k)], sem_us.at[i]))
+            by_count([dev for dev, _ in OWNER[f]], lambda k: drained(u_send[f].at[pl.ds(0, total - k)], sem_load.at[1 + i]))
 
     def stage_c(p):
         f, j0, jm, j1 = PIECES[p]
@@ -244,7 +246,7 @@
             rf, r0, _, r1 = PIECES[ready]
             for j in range(r0, r1):
                 dev, slot = OWNER[rf][j]
-                copy = remote(u_send[rf].at[j], u_own[rf].at[slot, d], sem_us.at[fams.index(rf)],
+                copy = remote(u_send[rf].at[j], u_own[rf].at[slot, d], sem_load.at[1 + fams.index(rf)],
                               sem_ur.at[SLOT[rf] + slot], dev)
                 pl.when(d != dev)(copy.start)
         if j1 > sq_count:
@@ -433,7 +435,7 @@
         mine = full[f].at[pl.ds(j0, j1 - j0), d]
         send(mine, mine, sem_gs.at[fams.index(f)], sem_gr.at[q, 0], right)
         send(mine, mine, sem_gs.at[fams.index(f)], sem_gr.at[q, 0], left)
-        send(mine, mine, sem_gs.at[fams.index(f)], sem_gr.at[q, 2], peer)
+        send(mine, mine, sem_gs.at[fams.index(f)], sem_last.at[LAST[q]], peer)
 
     def stage_e(q):
         f, j0, jm, j1 = GROUPS[q]
@@ -441,18 +443,19 @@
         arrived(full[f].at[r, pl.ds(0, 2)], sem_gr.at[q, 0])
         for near, half_r, dev in ((left, a, right), (right, b, left)):
             send(full[f].at[half_r, near], full[f].at[half_r, near], sem_gs.at[fams.index(f)], sem_gr.at[q, 1], dev)
-            send(full[f].at[r, near], full[f].at[r, near], sem_gs.at[fams.index(f)], sem_gr.at[q, 2], peer)
+            send(full[f].at[r, near], full[f].at[r, near], sem_gs.at[fams.index(f)], sem_last.at[LAST[q]], peer)
 
     def stage_h(q):
         f, j0, jm, j1 = GROUPS[q]
         block = full[f].at[pl.ds(j0, j1 - j0), 2 * xo + c]
         arrived(block, sem_gr.at[q, 1])
-        send(block, block, sem_gs.at[fams.index(f)], sem_gr.at[q, 2], peer)
-
-    def stage_z(q):
-        f, j0, jm, j1 = GROUPS[q]
-        r = pl.ds(j0, j1 - j0)
-        arrived(full[f].at[r, pl.ds(0, 4)], sem_gr.at[q, 2])
+        send(block, block, sem_gs.at[fams.index(f)], sem_last.at[LAST[q]], peer)
+
+    def stage_z(i):
+        parts = [GROUPS[q] for q in range(len(GROUPS)) if LAST[q] == i]
+        f, j0, _, _ = parts[0]
+        j1 = parts[-1][3]
+        arrived(full[f].at[pl.ds(j0, j1 - j0), pl.ds(0, 4)], sem_last.at[i])
         if j1 > sq_count:
             size = fk.shape[1]
             for i in range(j1 - sq_count):
@@ -508,7 +511,6 @@
     u_drained()
     pl.when(even)(lambda: given("u", 1))
     pl.when(jnp.logical_not(even))(lambda: given("w", 0))
-    stage_z(0)
     for q in (1, 2, 3):
         stage_h(q)
     for q in (4, 6, 5):
@@ -520,14 +522,13 @@
         given("s", 0)
         given("s", 1)
     pl.when(has_kv)(lambda: given("s", 2))
-    for q in (1, 2, 3):
-        stage_z(q)
+    stage_z(0)
     stage_h(4)
     stage_h(6)
-    stage_z(4)
-    stage_z(6)
+    stage_z(1)
+    stage_z(3)
     stage_h(5)
-    stage_z(5)
+    stage_z(2)
     for i, f in enumerate(fams):
         drained(full[f].at[:, pl.ds(0, n - 1)], sem_gs.at[i])
 
@@ -537,10 +538,7 @@
     copies = []
     for src, dst in zip(sources, results):
         count = dst.shape[0]
-        step = count if len(dst.shape) == 3 else max(1, count // 3)
-        for j in range(0, count, step):
-            r = pl.ds(j, step)
-            copies.append(pltpu.make_async_copy(src.at[r], dst.at[r], sem))
+        copies.append(pltpu.make_async_copy(src.at[pl.ds(0, count)], dst, sem))
     for copy in copies:
         copy.start()
     for copy in copies:
@@ -585,7 +583,7 @@
             + [pltpu.VMEM((n,) + up[1:], BF16), pltpu.VMEM((3, size, size), BF16),
                pltpu.VMEM((PIECES[0][3], nx) + up[1:], F32)]
             + [dma((6,)), dma((5,)), dma((4,)), dma((6,)), dma((4,)), dma((3,)), dma((pieces,)), dma((pieces,)),
-               dma((3,)), dma((7,)), dma((7,)), dma((groups,)), dma((3,)), dma((groups, 3))]
+               dma((7,)), dma((groups,)), dma((groups, 2)), dma((4,))]
         )
 
         def whole(shape):

time: 186 us -> 185 us (level)
  no operation moved by 1% of the time
where the time goes in v1:
time: 185 us
  Pallas kernels  185 us (100%)
    pallas_call x1, Pallas kernels, local_step(): pl.pallas_call(body, out_shape=[pltpu.VMEM(shape, dtype) for shape, dtype...  179 us
    pallas_call x1, Pallas kernels, local_step(): pl.pallas_call(write_kernel, out_shape=out_shape, in_specs=[inside] * 12,...  6.07 us

profile of v1, /device:TPU:81, one launch (start us, length us, event | category | flops | bytes accessed | tf_op | source)
XLA Modules:
  0.0 185.4 jit_solution(17274770327979692706)
XLA Ops:
  0.6 178.7 %muon.1 = (f32[15,32,256]{2,1,0:T(8,128)S(1)}, f32[12,32,256]{2,1,0:T(8,128)S(1)}, bf16[15,8,32,256]{3,2,1,0:T(8,128)(2,1)S(1)}, f32[12,32,64]{2,1,0:T(8,128)S(1...) custom-call(f32[12,4,2,32,256]{4,3,2,1,0:T(8,128)} %bitcast.16, ...), custom_call_target="tpu_custom_call" | custom-call | tf_op jit(solution)/shard_map/muon/pallas_call | solution.py:611
  179.3 6.1 %write.1 = (f32[12,32,256]{2,1,0:T(8,128)}, f32[12,32,256]{2,1,0:T(8,128)}, bf16[12,8,32,256]{3,2,1,0:T(8,128)(2,1)}, f32[12,32,64]{2,1,0:T(8,128)}, f32[12,32,6...) custom-call(f32[15,32,256]{2,1,0:T(8,128)S(1)} %get-tuple-element.36, ...), custom_call_target="tpu_custom_call" | custom-call | tf_op jit(solution)/shard_map/write/pallas_call | solution.py:621

commit v2 on v1

--- a/solution.py
+++ b/solution.py
@@ -28,6 +28,7 @@
 GROUPS = (
     ("u", 0, 2, 4), ("u", 4, 6, 8), ("u", 8, 10, 12), ("w", 0, 2, 4), ("w", 4, 5, 6), ("s", 0, 4, 8), ("s", 8, 11, 15),
 )
+OPP_SEMS, FIN_SEMS = 4, 5
 LAST = (0, 0, 0, 1, 1, 2, 3)
 OWNER = {
     "u": tuple((dev, 0) for dev in (0, 2, 4, 6, 1, 3, 5, 7)) + tuple((dev, 1) for dev in (0, 2, 4, 6)),
@@ -155,14 +156,14 @@
         a, b = pl.ds(j0, jm - j0), pl.ds(jm, j1 - jm)
 
         def send_opp():
-            send(pr.at[a, xo], opp[f].at[a], sem_st_s.at[fams.index(f)], sem_opp.at[p], right)
-            send(pr.at[b, xo], opp[f].at[b], sem_st_s.at[fams.index(f)], sem_opp.at[p], left)
+            send(pr.at[a, xo], opp[f].at[a], sem_st_s.at[fams.index(f)], sem_opp.at[p % OPP_SEMS], right)
+            send(pr.at[b, xo], opp[f].at[b], sem_st_s.at[fams.index(f)], sem_opp.at[p % OPP_SEMS], left)
 
         def send_right():
-            send(pr.at[b, xr], from_l[f].at[b], sem_st_s.at[fams.index(f)], sem_fin.at[p], right)
+            send(pr.at[b, xr], from_l[f].at[b], sem_st_s.at[fams.index(f)], sem_fin.at[p % FIN_SEMS], right)
 
         def send_left():
-            send(pr.at[a, xl], from_r[f].at[a], sem_st_s.at[fams.index(f)], sem_fin.at[p], left)
+            send(pr.at[a, xl], from_r[f].at[a], sem_st_s.at[fams.index(f)], sem_fin.at[p % FIN_SEMS], left)
 
         if p == 0:
             for i, (to, then) in enumerate(((xo, send_opp), (xr, send_right), (xl, send_left), (x, None))):
@@ -201,7 +202,7 @@
     def stage_b(p):
         f, j0, jm, j1 = PIECES[p]
         op, pr = opp[f], part[f]
-        arrived(op.at[pl.ds(j0, j1 - j0)], sem_opp.at[p])
+        arrived(op.at[pl.ds(j0, j1 - j0)], sem_opp.at[p % OPP_SEMS])
         for lo, hi, to, dev, dst in ((j0, jm, xr, right, from_l), (jm, j1, xl, left, from_r)):
             r = pl.ds(lo, hi - lo)
 
@@ -209,7 +210,7 @@
                 op[j] = op[j] + pr[j, to]
                 return carry
             lax.fori_loop(lo, hi, add, 0)
-            send(op.at[r], dst[f].at[r], sem_st_s.at[fams.index(f)], sem_fin.at[p], dev)
+            send(op.at[r], dst[f].at[r], sem_st_s.at[fams.index(f)], sem_fin.at[p % FIN_SEMS], dev)
 
     def by_count(devs, fn):
         counts = [devs.count(dev) for dev in range(n)]
@@ -228,7 +229,7 @@
     def stage_c(p):
         f, j0, jm, j1 = PIECES[p]
         need("mom_" + f)
-        arrived(part[f].at[pl.ds(j0, j1 - j0), pl.ds(0, 2)], sem_fin.at[p])
+        arrived(part[f].at[pl.ds(j0, j1 - j0), pl.ds(0, 2)], sem_fin.at[p % FIN_SEMS])
         if j1 > sq_count:
             loaded(mv_k, sem_mw.at[3])
             wide = m_kv.shape[2]
@@ -443,6 +444,7 @@
         arrived(full[f].at[r, pl.ds(0, 2)], sem_gr.at[q, 0])
         for near, half_r, dev in ((left, a, right), (right, b, left)):
             send(full[f].at[half_r, near], full[f].at[half_r, near], sem_gs.at[fams.index(f)], sem_gr.at[q, 1], dev)
+        for near in (left, right):
             send(full[f].at[r, near], full[f].at[r, near], sem_gs.at[fams.index(f)], sem_last.at[LAST[q]], peer)
 
     def stage_h(q):
@@ -538,7 +540,10 @@
     copies = []
     for src, dst in zip(sources, results):
         count = dst.shape[0]
-        copies.append(pltpu.make_async_copy(src.at[pl.ds(0, count)], dst, sem))
+        step = count if len(dst.shape) == 3 else max(1, count // 3)
+        for j in range(0, count, step):
+            r = pl.ds(j, step)
+            copies.append(pltpu.make_async_copy(src.at[r], dst.at[r], sem))
     for copy in copies:
         copy.start()
     for copy in copies:
@@ -582,7 +587,7 @@
             + per((), BF16) + own((3, 2, 2)) + per((), BF16)
             + [pltpu.VMEM((n,) + up[1:], BF16), pltpu.VMEM((3, size, size), BF16),
                pltpu.VMEM((PIECES[0][3], nx) + up[1:], F32)]
-            + [dma((6,)), dma((5,)), dma((4,)), dma((6,)), dma((4,)), dma((3,)), dma((pieces,)), dma((pieces,)),
+            + [dma((6,)), dma((5,)), dma((4,)), dma((6,)), dma((4,)), dma((3,)), dma((OPP_SEMS,)), dma((FIN_SEMS,)),
                dma((7,)), dma((groups,)), dma((groups, 2)), dma((4,))]
         )
 

time: 185 us -> 185 us (level)
  no operation moved by 1% of the time
where the time goes in v2:
time: 185 us
  Pallas kernels  185 us (100%)
    pallas_call x1, Pallas kernels, local_step(): pl.pallas_call(body, out_shape=[pltpu.VMEM(shape, dtype) for shape, dtype...  179 us
    pallas_call x1, Pallas kernels, local_step(): pl.pallas_call(write_kernel, out_shape=out_shape, in_specs=[inside] * 12,...  6.01 us

profile of v2, /device:TPU:81, one launch (start us, length us, event | category | flops | bytes accessed | tf_op | source)
XLA Modules:
  0.0 185.2 jit_solution(15506911047417865446)
XLA Ops:
  0.6 178.5 %muon.1 = (f32[15,32,256]{2,1,0:T(8,128)S(1)}, f32[12,32,256]{2,1,0:T(8,128)S(1)}, bf16[15,8,32,256]{3,2,1,0:T(8,128)(2,1)S(1)}, f32[12,32,64]{2,1,0:T(8,128)S(1...) custom-call(f32[12,4,2,32,256]{4,3,2,1,0:T(8,128)} %bitcast.16, ...), custom_call_target="tpu_custom_call" | custom-call | tf_op jit(solution)/shard_map/muon/pallas_call | solution.py:616
  179.2 6.0 %write.1 = (f32[12,32,256]{2,1,0:T(8,128)}, f32[12,32,256]{2,1,0:T(8,128)}, bf16[12,8,32,256]{3,2,1,0:T(8,128)(2,1)}, f32[12,32,64]{2,1,0:T(8,128)}, f32[12,32,6...) custom-call(f32[15,32,256]{2,1,0:T(8,128)S(1)} %get-tuple-element.36, ...), custom_call_target="tpu_custom_call" | custom-call | tf_op jit(solution)/shard_map/write/pallas_call | solution.py:626

commit v3 on v2

--- a/solution.py
+++ b/solution.py
@@ -112,17 +112,24 @@
     for i, to in enumerate((xo, xr, xl, x)):
         send(first.at[:, to], other[f0].at[r0, to], sem_peer_s.at[fams.index(f0)], sem_first.at[i], peer)
 
-    for p in range(1, len(PIECES)):
+    def begin(p):
         f, r = piece(p)
         load_part(p)
         send(grad[f].at[r, :, 1 - c], other[f].at[r], sem_peer_s.at[fams.index(f)],
              sem_peer_r.at[next(i for i, pieces in enumerate(PEER_SETS) if p in pieces)], peer)
-    pltpu.make_async_copy(g_kv, pk, sem_load.at[4]).start()
-    send(g_kv, qk, sem_peer_s.at[3], sem_peer_r.at[len(PEER_SETS)], peer)
+
     sq = pl.ds(0, sq_count)
-    for i, src, dst in ((0, m_up, mv_u), (0, w_up, wv_u), (1, m_dn, mv_w), (1, w_dn, wv_w),
-                        (2, m_sq, mv_s.at[sq]), (2, w_sq, wv_s), (3, m_kv, mv_k), (4, w_kv, wv_k)):
-        pltpu.make_async_copy(src, dst, sem_mw.at[i]).start()
+
+    def begin_rest():
+        for p in range(2, len(PIECES)):
+            begin(p)
+        pltpu.make_async_copy(g_kv, pk, sem_load.at[4]).start()
+        send(g_kv, qk, sem_peer_s.at[3], sem_peer_r.at[len(PEER_SETS)], peer)
+        for i, src, dst in ((0, m_up, mv_u), (0, w_up, wv_u), (1, m_dn, mv_w), (1, w_dn, wv_w),
+                            (2, m_sq, mv_s.at[sq]), (2, w_sq, wv_s), (3, m_kv, mv_k), (4, w_kv, wv_k)):
+            pltpu.make_async_copy(src, dst, sem_mw.at[i]).start()
+
+    begin(1)
     first_n = PIECES[0][3]
     pending = {
         "load_u": lambda: loaded(part["u"].at[pl.ds(first_n, p_u.shape[0] - first_n)], sem_load.at[1]),
@@ -493,6 +500,8 @@
     for i in range(-2, count):
         if i + 2 < count:
             stage_a(i + 2)
+        if i == -2:
+            begin_rest()
         if 0 <= i + 1 < count:
             stage_b(i + 1)
         if i >= 0:
@@ -529,10 +538,11 @@
     stage_h(6)
     stage_z(1)
     stage_z(3)
+    for i in (0, 1):
+        drained(full[fams[i]].at[:, pl.ds(0, n - 1)], sem_gs.at[i])
     stage_h(5)
     stage_z(2)
-    for i, f in enumerate(fams):
-        drained(full[f].at[:, pl.ds(0, n - 1)], sem_gs.at[i])
+    drained(full["s"].at[:, pl.ds(0, n - 1)], sem_gs.at[2])
 
 
 def write_kernel(*refs):

time: 185 us -> 185 us (level)
  no operation moved by 1% of the time
where the time goes in v3:
time: 185 us
  Pallas kernels  185 us (100%)
    pallas_call x1, Pallas kernels, local_step(): pl.pallas_call(body, out_shape=[pltpu.VMEM(shape, dtype) for shape, dtype...  179 us
    pallas_call x1, Pallas kernels, local_step(): pl.pallas_call(write_kernel, out_shape=out_shape, in_specs=[inside] * 12,...  6.01 us

profile of v3, /device:TPU:81, one launch (start us, length us, event | category | flops | bytes accessed | tf_op | source)
XLA Modules:
  0.0 185.2 jit_solution(13845711429762101155)
XLA Ops:
  0.6 178.5 %muon.1 = (f32[15,32,256]{2,1,0:T(8,128)S(1)}, f32[12,32,256]{2,1,0:T(8,128)S(1)}, bf16[15,8,32,256]{3,2,1,0:T(8,128)(2,1)S(1)}, f32[12,32,64]{2,1,0:T(8,128)S(1...) custom-call(f32[12,4,2,32,256]{4,3,2,1,0:T(8,128)} %bitcast.16, ...), custom_call_target="tpu_custom_call" | custom-call | tf_op jit(solution)/shard_map/muon/pallas_call | solution.py:626
  179.2 6.0 %write.1 = (f32[12,32,256]{2,1,0:T(8,128)}, f32[12,32,256]{2,1,0:T(8,128)}, bf16[12,8,32,256]{3,2,1,0:T(8,128)(2,1)}, f32[12,32,64]{2,1,0:T(8,128)}, f32[12,32,6...) custom-call(f32[15,32,256]{2,1,0:T(8,128)S(1)} %get-tuple-element.36, ...), custom_call_target="tpu_custom_call" | custom-call | tf_op jit(solution)/shard_map/write/pallas_call | solution.py:636

commit v4 on v3

--- a/solution.py
+++ b/solution.py
@@ -109,8 +109,11 @@
     load_part(0)
     pl.semaphore_wait(barrier, 3)
     loaded(first, sem_load.at[5])
-    for i, to in enumerate((xo, xr, xl, x)):
-        send(first.at[:, to], other[f0].at[r0, to], sem_peer_s.at[fams.index(f0)], sem_first.at[i], peer)
+    rows = first.shape[2]
+    upper, lower, both = pl.ds(0, rows // 2), pl.ds(rows // 2, rows // 2), pl.ds(0, rows)
+    first_parts = ((xo, upper), (xo, lower), (xr, both), (xl, both), (x, both))
+    for i, (to, lines) in enumerate(first_parts):
+        send(first.at[:, to, lines], other[f0].at[r0, to, lines], sem_peer_s.at[fams.index(f0)], sem_first.at[i], peer)
 
     def begin(p):
         f, r = piece(p)
@@ -173,15 +176,18 @@
             send(pr.at[a, xl], from_r[f].at[a], sem_st_s.at[fams.index(f)], sem_fin.at[p % FIN_SEMS], left)
 
         if p == 0:
-            for i, (to, then) in enumerate(((xo, send_opp), (xr, send_right), (xl, send_left), (x, None))):
-                arrived(ot.at[pl.ds(j0, j1 - j0), to], sem_first.at[i])
+            for i, (to, lines) in enumerate(first_parts):
+                arrived(ot.at[pl.ds(j0, j1 - j0), to, lines], sem_first.at[i])
 
                 def add_first(j, carry):
-                    pr[j, to] = pr[j, to] + ot[j, to]
+                    pr[j, to, lines] = pr[j, to, lines] + ot[j, to, lines]
                     return carry
                 lax.fori_loop(j0, j1, add_first, 0)
-                if then is not None:
-                    then()
+                if i < 2:
+                    send(pr.at[a, xo, lines], opp[f].at[a, lines], sem_st_s.at[fams.index(f)], sem_opp.at[p % OPP_SEMS], right)
+                    send(pr.at[b, xo, lines], opp[f].at[b, lines], sem_st_s.at[fams.index(f)], sem_opp.at[p % OPP_SEMS], left)
+                elif i < 4:
+                    (send_right, send_left)[i - 2]()
             return
         need(next(pieces for pieces in PEER_SETS if p in pieces))
         if f == "s":
@@ -597,7 +603,7 @@
             + per((), BF16) + own((3, 2, 2)) + per((), BF16)
             + [pltpu.VMEM((n,) + up[1:], BF16), pltpu.VMEM((3, size, size), BF16),
                pltpu.VMEM((PIECES[0][3], nx) + up[1:], F32)]
-            + [dma((6,)), dma((5,)), dma((4,)), dma((6,)), dma((4,)), dma((3,)), dma((OPP_SEMS,)), dma((FIN_SEMS,)),
+            + [dma((6,)), dma((5,)), dma((4,)), dma((6,)), dma((5,)), dma((3,)), dma((OPP_SEMS,)), dma((FIN_SEMS,)),
                dma((7,)), dma((groups,)), dma((groups, 2)), dma((4,))]
         )
 

time: 185 us -> 185 us (level)
  no operation moved by 1% of the time
where the time goes in v4:
time: 185 us
  Pallas kernels  184 us (99%)
    pallas_call x1, Pallas kernels, local_step(): pl.pallas_call(body, out_shape=[pltpu.VMEM(shape, dtype) for shape, dtype...  178 us
    pallas_call x1, Pallas kernels, local_step(): pl.pallas_call(write_kernel, out_shape=out_shape, in_specs=[inside] * 12,...  6.01 us

profile of v4, /device:TPU:81, one launch (start us, length us, event | category | flops | bytes accessed | tf_op | source)
XLA Modules:
  0.0 185.0 jit_solution(14107365943696261903)
XLA Ops:
  0.6 178.3 %muon.1 = (f32[15,32,256]{2,1,0:T(8,128)S(1)}, f32[12,32,256]{2,1,0:T(8,128)S(1)}, bf16[15,8,32,256]{3,2,1,0:T(8,128)(2,1)S(1)}, f32[12,32,64]{2,1,0:T(8,128)S(1...) custom-call(f32[12,4,2,32,256]{4,3,2,1,0:T(8,128)} %bitcast.16, ...), custom_call_target="tpu_custom_call" | custom-call | tf_op jit(solution)/shard_map/muon/pallas_call | solution.py:632
  179.0 6.0 %write.1 = (f32[12,32,256]{2,1,0:T(8,128)}, f32[12,32,256]{2,1,0:T(8,128)}, bf16[12,8,32,256]{3,2,1,0:T(8,128)(2,1)}, f32[12,32,64]{2,1,0:T(8,128)}, f32[12,32,6...) custom-call(f32[15,32,256]{2,1,0:T(8,128)S(1)} %get-tuple-element.36, ...), custom_call_target="tpu_custom_call" | custom-call | tf_op jit(solution)/shard_map/write/pallas_call | solution.py:642
